TPU v7x, 8 devices: a whole 2x2x1 slice. The times are simulated.
8 devices in a mesh: sp: 8 (over z, y, x, core).
Axes of the slice: x: 2, y: 2, z: 1, core: 2. Of those that a mesh axis runs over, the one named last changes fastest.
Arguments:
- hidden: bfloat16 [16, 1024, 2048], P(None, 'sp')
- d_out: bfloat16 [16, 1024, 2048], P(None, 'sp')
- w_query: bfloat16 [2048, 8, 256], replicated
- w_key: bfloat16 [2048, 256], replicated
- w_value: bfloat16 [2048, 256], replicated
- w_out: bfloat16 [8, 256, 2048], replicated
Outputs:
- output 1: bfloat16 [16, 1024, 2048], P(None, 'sp')
- output 2: bfloat16 [16, 1024, 2048], P(None, 'sp')
- output 3: float32 [2048, 8, 256], replicated
- output 4: float32 [2048, 256], replicated
- output 5: float32 [2048, 256], replicated
- output 6: float32 [8, 256, 2048], replicated
All inputs are finite; a program needn't handle non-finite values.
Results may differ from a plain program's by a relative error of at most 0.0193.
Values are sent between devices in bfloat16 or wider.
A program may use at most 1 GiB of HBM per device.

v0:
```python
import functools

import jax
import jax.numpy as jnp
from jax import lax
from jax.experimental import pallas as pl
from jax.experimental.pallas import tpu as pltpu
from jax.sharding import PartitionSpec as P

F32 = jnp.float32
BF16 = jnp.bfloat16
NT = (((1,), (1,)), ((), ()))
NN = (((1,), (0,)), ((), ()))
TN = (((0,), (0,)), ((), ()))
LOG2E = 1.4426950408889634
CHIP_BLOCKS = ((0,), (0, 1), (0, 2, 3), (0, 1, 2, 3))


def dot(a, b, dims):
    return lax.dot_general(a, b, dims, preferred_element_type=F32)


def rope_tables(positions, head_dim):
    half_dim = head_dim // 2
    inv_freq = 10000.0 ** (-(jnp.arange(half_dim).astype(F32) * 2.0) / head_dim)
    angles = positions.astype(F32)[:, None] * inv_freq[None, :]
    return jnp.cos(angles), jnp.sin(angles)


def rotate(x, cos, sin, sign):
    half = x.shape[-1] // 2
    a, b = x[..., :half].astype(F32), x[..., half:].astype(F32)
    s = sin * sign
    return jnp.concatenate([a * cos - b * s, b * cos + a * s], axis=-1).astype(BF16)


def attn_step(blocks, heads, hd, scale, core, first, s, step, q_refs, do_refs, kv, k_rot, cos_ref, sin_ref, stage, slot, acc):
    rows = kv.shape[2]
    half_rows = rows // 2
    flip = core * half_rows
    pos = lambda t: jnp.where(t < half_rows, t + flip, t - flip)
    cos, sin = cos_ref[:rows], sin_ref[:rows]

    @pl.when(first)
    def _():
        for b in blocks:
            tab = slice(b * rows, (b + 1) * rows)
            k_rot[b] = rotate(kv[b, s, :, :hd], cos_ref[tab], sin_ref[tab], 1.0)

    keep = pos(lax.broadcasted_iota(jnp.int32, (rows, rows), 0)) >= pos(lax.broadcasted_iota(jnp.int32, (rows, rows), 1))
    for h in range(heads):
        cols = slice(h * hd, (h + 1) * hd)
        wide = pl.ds(pl.multiple_of((step * heads + h) * hd, hd), hd)
        q = rotate(jnp.concatenate([q_refs[0][0, :, cols], q_refs[1][s, :, wide]], axis=0), cos, sin, 1.0)
        do = jnp.concatenate([do_refs[0][0, :, cols], do_refs[1][s, :, wide]], axis=0)
        sc = [dot(q, k_rot[b], NT) for b in blocks]
        sc[0] = jnp.where(keep, sc[0], -jnp.inf)
        m = functools.reduce(jnp.maximum, [jnp.max(t, axis=1, keepdims=True) for t in sc])
        e = [jnp.exp2((t - m) * (scale * LOG2E)) for t in sc]
        inv = 1.0 / functools.reduce(jnp.add, [jnp.sum(t, axis=1, keepdims=True) for t in e])
        p = [t * inv for t in e]
        pb = [t.astype(BF16) for t in p]
        o = functools.reduce(jnp.add, [dot(pb[i], kv[b, s, :, hd:], NN) for i, b in enumerate(blocks)]).astype(BF16)
        stage[slot, 0, 0, :, wide] = o[:half_rows]
        stage[slot, 0, 1, :, wide] = o[half_rows:]
        delta = jnp.sum(do.astype(F32) * o.astype(F32), axis=1, keepdims=True)
        ds = [(p[i] * (dot(do, kv[b, s, :, hd:], NT) - delta) * scale).astype(BF16) for i, b in enumerate(blocks)]
        dq = functools.reduce(jnp.add, [dot(ds[i], k_rot[b], NN) for i, b in enumerate(blocks)]).astype(BF16)
        dq = rotate(dq, cos, sin, -1.0)
        stage[slot, 1, 0, :, wide] = dq[:half_rows]
        stage[slot, 1, 1, :, wide] = dq[half_rows:]
        for i, b in enumerate(blocks):
            dk = dot(ds[i], q, TN)
            dv = dot(pb[i], do, TN)
            if h == 0:
                @pl.when(first)
                def _():
                    acc[b, s, :, :hd] = dk
                    acc[b, s, :, hd:] = dv

                @pl.when(jnp.logical_not(first))
                def _():
                    acc[b, s, :, :hd] += dk
                    acc[b, s, :, hd:] += dv
            else:
                acc[b, s, :, :hd] += dk
                acc[b, s, :, hd:] += dv


MESH = pl.DeviceIdType.MESH
PIECE = 512


def remote(src, dst, sems, i, dev):
    return pltpu.make_async_remote_copy(src_ref=src, dst_ref=dst, send_sem=sems.at[0, i], recv_sem=sems.at[1, i], device_id=(dev,), device_id_type=MESH)


def sum_kernel(counts, *refs):
    ng = len(counts)
    hid_ref, dout_ref, o_ref, wo_ref, dq_ref, wq_ref, dkv_ref, wkv_ref = refs[:8]
    out_refs, (attn_out, d_hidden, dr) = refs[8:ng + 8], refs[ng + 8:ng + 11]
    h, dv, give, flip, r1, r2, xs, ws, xs2, ws2, tiles, dr_sem, mm_sem, tile_sem, keep_sem, d_sem, s1_sem, s2_sem, g1_sem, g2_sem, g3_sem = refs[ng + 11:]
    total = sum(counts)
    dev = lax.axis_index('sp')
    chip, core = dev // 2, dev % 2
    bits = (chip % 2, chip // 2)
    partner = dev + 1 - 2 * core
    across = (dev + 2 - 4 * bits[0], dev + 4 - 8 * bits[1])
    half, quarter, eighth, last = PIECE // 2, PIECE // 4, PIECE // 8, PIECE // 16

    barrier = pltpu.get_barrier_semaphore()
    for d in (partner,) + across:
        pl.semaphore_signal(barrier, inc=1, device_id=(d,), device_id_type=MESH)
    pl.semaphore_wait(barrier, 3)

    def rows(ref, start, size):
        return ref.at[pl.ds(pl.multiple_of(start, 32), size)]

    def each(body, which=range(ng)):
        base = 0
        for i, count in enumerate(counts):
            def step(p, carry, i=i, base=base):
                body(i, p, base + p)
                return carry
            if i in which:
                lax.fori_loop(0, count, step, 0)
            base += count

    def cross(s):
        return remote(give.at[s % 2], dr.at[s], d_sem, s, partner)

    def first(w, s):
        src = h.at[s, pl.ds(pl.multiple_of(w * quarter + (1 - bits[w]) * eighth, 32), eighth)]
        return remote(src, r1.at[w, s], s1_sem.at[w], s, across[w])

    def second(w, s):
        src = h.at[s, pl.ds(pl.multiple_of(w * quarter + bits[w] * eighth + (1 - bits[1 - w]) * last, 32), last)]
        return remote(src, r2.at[w, s], s2_sem.at[w], s, across[1 - w])

    def kept(w):
        return w * quarter + bits[w] * eighth

    def final(w):
        return kept(w) + bits[1 - w] * last

    def keep(w, i, p, s):
        return pltpu.make_async_copy(h.at[s, pl.ds(pl.multiple_of(final(w), 32), last)], rows(out_refs[i], p * PIECE + core * half + final(w), last), keep_sem.at[w, s])

    def share1(w, i, p, s):
        return remote(h.at[s, pl.ds(pl.multiple_of(final(w), 32), last)], rows(out_refs[i], p * PIECE + core * half + final(w), last), g1_sem.at[w], s, across[1 - w])

    def share2(w, i, p, s):
        here = rows(out_refs[i], p * PIECE + core * half + kept(w), eighth)
        return remote(here, here, g2_sem.at[w], s, across[w])

    def share3(i, p, s):
        here = rows(out_refs[i], p * PIECE + core * half, half)
        return remote(here, here, g3_sem, s, partner)

    def product_rows(left, right, start, put):
        cols = pl.ds(pl.multiple_of(start, half), half)

        @pl.loop(0, left.shape[0], step=half)
        def _(r):
            at = pl.ds(pl.multiple_of(r, half), half)
            flip[:, at] = left[at, cols].T

        @pl.loop(0, right.shape[1], step=512)
        def _(c):
            at = pl.ds(pl.multiple_of(c, 512), 512)
            put(at, dot(flip[...], right[:, at], NN))

    def phase1(left, right, i, p, s):
        @pl.when(s >= 2)
        def _():
            cross(s - 2).wait_send()

        def put_give(at, x):
            give[s % 2, :, at] = x

        def put_keep(at, x):
            h[s, :, at] = x
        product_rows(left, right, p * PIECE + (1 - core) * half, put_give)
        cross(s).start()
        product_rows(left, right, p * PIECE + core * half, put_keep)
        cross(s).wait_recv()
        fetch = pltpu.make_async_copy(dr.at[s], dv, dr_sem)
        fetch.start()
        fetch.wait()

        @pl.loop(0, half, step=32)
        def _(r):
            at = pl.ds(pl.multiple_of(r, 32), 32)
            h[s, at] += dv[at]
        for w in range(2):
            first(w, s).start()

    def phase2(i, p, s):
        for w in range(2):
            first(w, s).wait()
            at = pl.ds(pl.multiple_of(kept(w), 32), eighth)
            h[s, at] += r1[w, s]
            second(w, s).start()

    def phase3(i, p, s):
        for w in range(2):
            second(w, s).wait()
            at = pl.ds(pl.multiple_of(final(w), 32), last)
            h[s, at] += r2[w, s]
            share1(w, i, p, s).start()
            keep(w, i, p, s).start()

    def phase4(i, p, s):
        for w in range(2):
            share1(w, i, p, s).wait()
            keep(w, i, p, s).wait()
            share2(w, i, p, s).start()

    def phase5(i, p, s):
        for w in range(2):
            share2(w, i, p, s).wait()
        share3(i, p, s).start()

    def phase6(i, p, s):
        share3(i, p, s).wait()

    tm, tn = tiles.shape[1:]
    across_n = ws.shape[0] // tn
    n_tiles = xs.shape[0] // tm * across_n

    def bring(src, dst, k):
        return pltpu.make_async_copy(src, dst, mm_sem.at[k])

    def spill(out, t):
        at = (pl.ds(pl.multiple_of(t // across_n * tm, tm), tm), pl.ds(pl.multiple_of(t % across_n * tn, tn), tn))
        return pltpu.make_async_copy(tiles.at[t % 2], out.at[at], tile_sem.at[t % 2])

    def matmul(out, product):
        @pl.loop(0, n_tiles)
        def _(t):
            @pl.when(t >= 2)
            def _():
                spill(out, t - 2).wait()
            m, c = pl.ds(pl.multiple_of(t // across_n * tm, tm), tm), pl.ds(pl.multiple_of(t % across_n * tn, tn), tn)
            tiles[t % 2] = product(m, c).astype(BF16)
            spill(out, t).start()
        for t in (n_tiles - 2, n_tiles - 1):
            spill(out, t).wait()

    def forward(m, c):
        return dot(ws[m], xs[:, c], NN)

    def backward(m, c):
        return dot(ws[m], xs[c], NT) + dot(xs2[m], ws2[c], NT)

    def bring_all(*pairs):
        copies = [bring(src, dst, k) for k, (src, dst) in enumerate(pairs)]
        for copy in copies:
            copy.start()
        for copy in copies:
            copy.wait()

    bring_all((o_ref, xs), (dout_ref, ws))
    each(functools.partial(phase1, xs, ws), (0,))
    bring_all((hid_ref, xs), (dq_ref, ws), (dkv_ref, xs2), (wkv_ref, ws2))
    each(functools.partial(phase1, xs, ws), (1,))
    each(functools.partial(phase1, xs2, xs), (2,))
    for s in (total - 2, total - 1):
        cross(s).wait_send()
    bring_all((wq_ref, xs))
    each(phase2, (0,))
    matmul(d_hidden, backward)
    each(phase2, (1, 2))
    bring_all((o_ref, ws), (wo_ref, xs))
    each(phase3, (0,))
    matmul(attn_out, forward)
    each(phase3, (1, 2))
    for phase in (phase4, phase5, phase6):
        each(phase)


def sum_all(hidden, d_out, o, wo, dq, wq, dkv, wkv):
    grads = [(o.shape[1], d_out.shape[1]), (hidden.shape[1], dq.shape[1]), (dkv.shape[1], hidden.shape[1])]
    counts = tuple(g[0] // PIECE for g in grads)
    total = sum(counts)
    width = grads[0][1]
    dma = pltpu.SemaphoreType.DMA
    hbm = pl.BlockSpec(memory_space=pl.ANY)
    act = jax.ShapeDtypeStruct((o.shape[0], wo.shape[1]), BF16)
    res = pl.pallas_call(
        functools.partial(sum_kernel, counts),
        out_shape=[jax.ShapeDtypeStruct(g, F32) for g in grads] + [act, act, jax.ShapeDtypeStruct((total, PIECE // 2, width), F32)],
        in_specs=[hbm] * 8,
        out_specs=[hbm] * (len(grads) + 3),
        scratch_shapes=[
            pltpu.VMEM((total, PIECE // 2, width), F32),
            pltpu.VMEM((PIECE // 2, width), F32),
            pltpu.VMEM((2, PIECE // 2, width), F32),
            pltpu.VMEM((PIECE // 2, o.shape[0]), BF16),
            pltpu.VMEM((2, total, PIECE // 8, width), F32),
            pltpu.VMEM((2, total, PIECE // 16, width), F32),
            pltpu.VMEM(o.shape, BF16), pltpu.VMEM(wo.shape, BF16),
            pltpu.VMEM(dkv.shape, BF16), pltpu.VMEM(wkv.shape, BF16),
            pltpu.VMEM((2, 512, 256), BF16),
            dma, dma((4,)), dma((2,)), dma((2, total)), dma((2, total)),
            dma((2, 2, total)), dma((2, 2, total)), dma((2, 2, total)), dma((2, 2, total)), dma((2, total)),
        ],
        compiler_params=pltpu.CompilerParams(collective_id=1, has_side_effects=True, vmem_limit_bytes=67 * 1000 * 1000),
        name="sum_all",
    )(hidden, d_out, o, wo, dq, wq, dkv, wkv)
    return res[:-1]


def attn_kernel(heads, hd, lag, q_mine, do_mine, q_all, do_all, kv_all, cos_ref, sin_ref, o_out, dq_out, dkv_out,
                kv, k_rot, q_in, do_in, stage, acc, relay, got, kv_mine_sem, pair_sem, kv_sem, in_sem, keep_sem, give_sem, one_sem, two_sem):
    s, step = pl.program_id(0), pl.program_id(1)
    steps = pl.num_programs(1)
    ns, rows = kv.shape[1], kv.shape[2]
    half_rows = rows // 2
    dev = lax.axis_index('sp')
    chip, core = dev // 2, dev % 2
    bit_x, bit_y = chip % 2, chip // 2
    partner = dev + 1 - 2 * core
    dev_x, dev_y = dev + 2 - 4 * bit_x, dev + 4 - 8 * bit_y
    dev_d = dev_x + 4 - 8 * bit_y
    mine, yours = core * ns, (1 - core) * ns
    slot = s % 2

    def give_kv(b, i):
        return remote(kv.at[0, i], kv.at[b, i], kv_sem.at[b - 1], i, (dev_x, dev_y, dev_d)[b - 1])

    def give_in(i, k):
        return remote((q_all, do_all)[k].at[yours + i], (q_in, do_in)[k].at[i], in_sem.at[k], i, partner)

    up = (bit_x == 0, bit_y == 0, bit_y == 0)
    down = (bit_x == 1, bit_y == 1, bit_y == 1)

    def pair():
        return remote(kv_all.at[pl.ds(yours, ns)], kv.at[0, :, pl.ds(half_rows, half_rows)], pair_sem, 0, partner)

    def own():
        return pltpu.make_async_copy(kv_all.at[pl.ds(mine, ns)], kv.at[0, :, pl.ds(0, half_rows)], kv_mine_sem)

    @pl.when((s == 0) & (step == 0))
    def _():
        barrier = pltpu.get_barrier_semaphore()
        for d in (partner, dev_x, dev_y, dev_d):
            pl.semaphore_signal(barrier, inc=1, device_id=(d,), device_id_type=MESH)
        pl.semaphore_wait(barrier, 4)
        pair().start()
        own().start()
        for k in range(2):
            give_in(0, k).start()
        own().wait()
        pair().wait()

        @pl.loop(0, ns)
        def _(i):
            for b in (1, 2, 3):
                @pl.when(up[b - 1])
                def _():
                    give_kv(b, i).start()

            @pl.when(i > 0)
            def _():
                for k in range(2):
                    give_in(i, k).start()

    def keep(i, k):
        return pltpu.make_async_copy(stage.at[i % 2, k, 0], (o_out, dq_out)[k].at[mine + i], keep_sem.at[k, i % 2])

    def give(i, k):
        return remote(stage.at[i % 2, k, 1], (o_out, dq_out)[k].at[mine + i], give_sem.at[k], i, partner)

    @pl.when(step == 0)
    def _():
        for k in range(2):
            give_in(s, k).wait()
        for b in (1, 2, 3):
            @pl.when(down[b - 1])
            def _():
                give_kv(b, s).wait_recv()

        @pl.when(s >= 2)
        def _():
            for k in range(2):
                keep(s - 2, k).wait()
                give(s - 2, k).wait_send()

    first = step == 0
    for c, blocks in enumerate(CHIP_BLOCKS):
        @pl.when(chip == c)
        def _():
            attn_step(blocks, heads, hd, hd ** -0.5, core, first, s, step, (q_mine, q_in), (do_mine, do_in), kv, k_rot, cos_ref, sin_ref, stage, slot, acc)

    def one(i, w):
        return remote(acc.at[3, i], relay.at[i], one_sem, i, (dev_x, dev_y)[w])

    def two(i, w):
        return remote(acc.at[1 + w, i], got.at[w, i], two_sem.at[w], i, (dev_x, dev_y)[w])

    def send_one(i):
        for w in range(2):
            @pl.when((bit_y == 1) & (i % 2 == w))
            def _():
                one(i, w).start()

    def send_two(i):
        even = i % 2 == 0
        @pl.when(even & (bit_y == 1))
        def _():
            one(i, 0).wait_recv()
            acc[2, i] += relay[i]

        @pl.when(jnp.logical_not(even) & (chip == 1))
        def _():
            one(i, 1).wait_recv()
            acc[1, i] += relay[i]

        @pl.when(jnp.logical_not(even) & (chip == 0))
        def _():
            one(i, 1).wait_recv()
            acc[1, i] = relay[i]

        @pl.when((bit_x == 1) | ((chip == 0) & jnp.logical_not(even)))
        def _():
            two(i, 0).start()

        @pl.when(bit_y == 1)
        def _():
            two(i, 1).start()

    def finish(i):
        even = i % 2 == 0

        @pl.when((bit_x == 0) | ((chip == 1) & jnp.logical_not(even)))
        def _():
            two(i, 0).wait_recv()
            acc[0, i] += got[0, i]

        @pl.when(bit_y == 0)
        def _():
            two(i, 1).wait_recv()
            acc[0, i] += got[1, i]
        total = acc[0, i].astype(BF16)
        dkv_out[i, :, :hd] = rotate(total[:, :hd], cos_ref[:rows], sin_ref[:rows], -1.0)
        dkv_out[i, :, hd:] = total[:, hd:]

    @pl.when(step == steps - 1)
    def _():
        for k in range(2):
            keep(s, k).start()
            give(s, k).start()
        send_one(s)

        @pl.when(s >= lag)
        def _():
            send_two(s - lag)

    @pl.when((s == ns - 1) & (step == steps - 1))
    def _():
        @pl.loop(ns - lag, ns)
        def _(i):
            send_two(i)

        @pl.loop(0, ns)
        def _(i):
            finish(i)
            for k in range(2):
                give(i, k).wait_recv()
            for b in (1, 2, 3):
                @pl.when(up[b - 1])
                def _():
                    give_kv(b, i).wait_send()
            for w in range(2):
                @pl.when((bit_y == 1) & (i % 2 == w))
                def _():
                    one(i, w).wait_send()

            @pl.when((bit_x == 1) | ((chip == 0) & (i % 2 == 1)))
            def _():
                two(i, 0).wait_send()

            @pl.when(bit_y == 1)
            def _():
                two(i, 1).wait_send()
        for i in (ns - 2, ns - 1):
            for k in range(2):
                keep(i, k).wait()
                give(i, k).wait_send()


def attention(q, do, kv, cos, sin, hd, heads=2, lag=1):
    batch, half_rows, width = q.shape
    ns, rows = batch // 2, 2 * half_rows
    mine = pl.BlockSpec((1, half_rows, heads * hd), lambda s, h: (lax.axis_index('sp') % 2 * ns + s, 0, h))
    tab = pl.BlockSpec((4 * rows, hd // 2), lambda s, h: (0, 0))
    hbm = pl.BlockSpec(memory_space=pl.ANY)
    act = jax.ShapeDtypeStruct(q.shape, BF16)
    dma = pltpu.SemaphoreType.DMA
    return pl.pallas_call(
        functools.partial(attn_kernel, heads, hd, lag),
        grid=(ns, width // (heads * hd)),
        in_specs=[mine, mine, hbm, hbm, hbm, tab, tab],
        out_specs=[hbm, hbm, pl.BlockSpec((ns, rows, 2 * hd), lambda s, h: (0, 0, 0))],
        out_shape=[act, act, jax.ShapeDtypeStruct((ns, rows, 2 * hd), BF16)],
        scratch_shapes=[
            pltpu.VMEM((4, ns, rows, 2 * hd), BF16),
            pltpu.VMEM((4, rows, hd), BF16),
            pltpu.VMEM((ns, half_rows, width), BF16),
            pltpu.VMEM((ns, half_rows, width), BF16),
            pltpu.VMEM((2, 2, 2, half_rows, width), BF16),
            pltpu.VMEM((4, ns, rows, 2 * hd), F32),
            pltpu.VMEM((ns, rows, 2 * hd), F32),
            pltpu.VMEM((2, ns, rows, 2 * hd), F32),
            dma, dma((2, 1)), dma((3, 2, ns)), dma((2, 2, ns)), dma((2, 2)), dma((2, 2, ns)), dma((2, ns)), dma((2, 2, ns)),
        ],
        compiler_params=pltpu.CompilerParams(dimension_semantics=("arbitrary", "arbitrary"), collective_id=2, has_side_effects=True, vmem_limit_bytes=66 * 1000 * 1000),
        cost_estimate=pl.CostEstimate(flops=6 * 2 * ns * rows * width * rows * 4, bytes_accessed=100 * 1024 * 1024, transcendentals=0),
        name="attention",
    )(q, do, q, do, kv, cos, sin)


def solution(mesh):
    n = mesh.shape['sp']
    seq_spec = P(None, 'sp', None)
    rep_spec = P()

    def local_step(hidden, d_out, w_query, w_key, w_value, w_out):
        batch, local_len, width = hidden.shape
        hd = w_key.shape[1]
        qw = w_query.shape[1] * hd
        dev = lax.axis_index('sp')
        core = dev % 2
        wq = w_query.reshape(width, qw)
        wo = w_out.reshape(qw, width)
        wkv = jnp.concatenate([w_key, w_value], axis=1)

        offset = jnp.arange(local_len)
        positions = [((dev ^ (2 * b)) ^ c) * local_len + offset for b in range(4) for c in range(2)]
        cos, sin = rope_tables(jnp.concatenate(positions), hd)

        proj = lambda x, w, eq: jnp.einsum(eq, x, w, preferred_element_type=F32).astype(BF16)
        kv = proj(hidden, wkv, 'bld,de->ble')
        do = proj(d_out, wo, 'bld,ed->ble')
        q = proj(hidden, wq, 'bld,de->ble')
        o, dq, dkv = attention(q, do, kv, cos, sin, hd)
        dkv_back = lax.ppermute(dkv[:, local_len:], 'sp', [(d, d ^ 1) for d in range(n)])

        dkv = dkv[:, :local_len]
        dkv = jnp.concatenate([jnp.where(core == 0, dkv, dkv_back), jnp.where(core == 0, dkv_back, dkv)], axis=0)
        flat = lambda x: x.reshape(batch * local_len, -1)
        grad_wo, grad_wq, grad_wkv, attn_out, d_hidden = sum_all(flat(hidden), flat(d_out), flat(o), wo, flat(dq), wq, flat(dkv), wkv)
        attn_out, d_hidden = attn_out.reshape(hidden.shape), d_hidden.reshape(hidden.shape)
        return (attn_out, d_hidden, grad_wq.reshape(w_query.shape), grad_wkv[:hd].T, grad_wkv[hd:].T, grad_wo.reshape(w_out.shape))

    return jax.shard_map(local_step, mesh=mesh, in_specs=(seq_spec, seq_spec, rep_spec, rep_spec, rep_spec, rep_spec), out_specs=(seq_spec, seq_spec, rep_spec, rep_spec, rep_spec, rep_spec), check_vma=False)
```

profile of v0, /device:TPU:0, one launch (start us, length us, event | category | flops | bytes accessed | tf_op | source)
XLA Modules:
  0.0 693.8 jit_solution(12362330380308532930)
XLA Ops:
  0.8 1.3 constant_dynamic-update-slice_fusion.1
  2.1 0.0 copy-start.2
  2.1 13.5 %reshape.113 = bf16[2048,2048,1]{1,0,2:T(8,128)(2,1)} reshape(bf16[2048,8,256]{2,1,0:T(8,128)(2,1)} %param.8) | data formatting | bytes 16777216 | tf_op jit(solution)/shard_map/reshape | solution.py:535
  15.6 0.0 copy-done.2
  15.7 0.1 constant_dynamic-update-slice_fusion.refs_7_
  15.7 0.0 copy-start
  15.8 0.0 slice-start.1
  15.8 0.0 slice-start.3
  15.8 9.9 %convert_bitcast_fusion.kv_all = bf16[16,128,512]{2,1,0:T(8,128)(2,1)} fusion(bf16[16,128,2048]{2,1,0:T(8,128)(2,1)} %param.6, bf16[2048,512]{1,0:T(8,128)(2,1)S(1)} %constant_dynamic-update-slice_fusion.refs_7_), kind=kOutput, calls=%fused_computation.7 | convolution fusion | flops 4296015872 | bytes 12582912 | tf_op jit(solution)/shard_map/bld,de->ble/dot_general | solution.py:543
  25.7 0.0 copy-done
  25.7 0.0 slice-done
  25.7 0.0 slice-done.2
  25.7 0.0 slice-done.1
  25.7 19.4 %convolution_convert_fusion.1.q_mine.q_all = bf16[16,128,2048]{2,1,0:T(8,128)(2,1)} fusion(bf16[16,128,2048]{2,1,0:T(8,128)(2,1)S(1)} %bitcast.42, bf16[2048,2048,1]{1,0,2:T(8,128)(2,1)S(1)} %bitcast.39), kind=kOutput, calls=%fused_computation.1 | convolution fusion | flops 17184063488 | bytes 25165824 | tf_op jit(solution)/shard_map/bld,de->ble/dot_general | solution.py:543
  45.2 3.0 multiply_sine_fusion
  48.2 23.7 %convolution_convert_fusion.do_mine.do_all = bf16[16,128,2048]{2,1,0:T(8,128)(2,1)} fusion(bf16[16,128,2048]{2,1,0:T(8,128)(2,1)} %param.7, bf16[2048,2048,1]{1,0,2:T(8,128)(2,1)} %bitcast.44), kind=kOutput, calls=%fused_computation | convolution fusion | flops 17184063488 | bytes 25165824 | tf_op jit(solution)/shard_map/bld,ed->ble/dot_general | solution.py:543
  71.9 227.5 %attention.1 = (bf16[16,128,2048]{2,1,0:T(8,128)(2,1)}, bf16[16,128,2048]{2,1,0:T(8,128)(2,1)}, bf16[8,256,512]{2,1,0:T(8,128)(2,1)}) custom-call(bf16[16,128,2048]{2,1,0:T(8,128)(2,1)} %convolution_convert_fusion.1.q_mine.q_all, bf16[16,128,2048]{2,1,0:T(8,128)(2,1)} %convolution_convert_fusion.do_mine.do_all, ...), custom_call_target="tpu_custom_call" | custom-call | flops 51539607552 | bytes 104857600 | tf_op jit(solution)/shard_map/attention/pallas_call | solution.py:501
  299.4 1.3 slice.13
  300.7 0.0 collective-permute-start
  300.8 0.0 copy-start.1
  300.8 10.6 %copy.16 = bf16[256,8,8,256]{3,1,2,0:T(8,128)(2,1)} copy(bf16[256,8,8,256]{3,2,1,0:T(8,128)(2,1)} %bitcast.31) | data formatting | bytes 16777216
  311.4 0.0 collective-permute-done
  311.4 0.1 broadcast_select_fusion.1
  311.5 1.5 pad_maximum_fusion
  313.0 327.1 %sum_all.1 = (f32[2048,2048]{1,0:T(8,128)}, f32[2048,2048]{1,0:T(8,128)}, f32[512,2048]{1,0:T(8,128)}, bf16[2048,2048]{1,0:T(8,128)(2,1)}, bf16[2048,2048]{1,0:T(8,128)(2,1)}, /*index=5*/f32[9,256,2048]{2,1,0:T(8,128)}) custom-call(bf16[2048,2048]{1,0:T(8,128)(2,1)} %bitcast.40, bf16[2048,2048]{1,0:T(8,128)(2,1)} %bitcast.43, bf16[2048,2048]{1,0:T(8,128)(2,1)} %bitcast.46, ...), custom_call_target="tpu_custom_call" | custom-call | tf_op jit(solution)/shard_map/sum_all/pallas_call | solution.py:290
  640.2 3.9 slice_bitcast_fusion
  644.1 2.9 copy.14
  647.0 1.8 copy.13
  648.8 15.9 %copy.17 = f32[256,8,8,256]{3,2,1,0:T(8,128)} copy(f32[256,8,8,256]{3,1,2,0:T(8,128)} %bitcast.34) | data formatting | bytes 33554432
  664.7 8.4 %copy.30 = bf16[16,128,2048]{2,1,0:T(8,128)(2,1)} copy(bf16[16,128,2048]{2,1,0:T(8,128)(2,1)} %bitcast.37) | data formatting | bytes 16777216
  673.1 8.5 %copy.31 = bf16[16,128,2048]{2,1,0:T(8,128)(2,1)} copy(bf16[16,128,2048]{2,1,0:T(8,128)(2,1)} %bitcast.36) | data formatting | bytes 16777216
  681.6 11.8 %copy.32 = f32[8,256,2048]{2,1,0:T(8,128)} copy(f32[8,256,2048]{2,1,0:T(8,128)} %bitcast.33) | data formatting | bytes 33554432
  (17 shorter events, 0.1 us)
Async XLA Ops:
  2.1 13.5 %copy-start.2 = (bf16[2048,256]{1,0:T(8,128)(2,1)S(1)}, bf16[2048,256]{1,0:T(8,128)(2,1)}, u32[]{:S(2)}) copy-start(bf16[2048,256]{1,0:T(8,128)(2,1)} %param.10) | copy-start | bytes 3145732
  15.6 10.1 %slice-start = ((s8[8388608]{0:T(1024)(128)(4,1)}), s8[4194304]{0:T(1024)(128)(4,1)S(1)}, s32[]{:S(2)}) async-start(s8[8388608]{0:T(1024)(128)(4,1)} %bitcast.38), calls=%async_computation | async-start | bytes 8388608
  15.6 10.1 %slice-start.2 = ((s8[8388608]{0:T(1024)(128)(4,1)}), s8[4194304]{0:T(1024)(128)(4,1)S(1)}, s32[]{:S(2)}) async-start(s8[8388608]{0:T(1024)(128)(4,1)} %bitcast.41), calls=%async_computation.2 | async-start | bytes 8388608
  15.7 10.0 %copy-start = (bf16[2048,512]{1,0:T(8,128)(2,1)}, bf16[2048,512]{1,0:T(8,128)(2,1)S(1)}, u32[]{:S(2)}) copy-start(bf16[2048,512]{1,0:T(8,128)(2,1)S(1)} %constant_dynamic-update-slice_fusion.refs_7_) | copy-start | bytes 6291460
  15.8 10.0 %slice-start.1 = ((s8[8388608]{0:T(1024)(128)(4,1)}), s8[4194304]{0:T(1024)(128)(4,1)S(1)}, s32[]{:S(2)}) async-start(s8[8388608]{0:T(1024)(128)(4,1)} %bitcast.38), calls=%async_computation.1 | async-start | bytes 8388608
  15.8 10.0 %slice-start.3 = ((s8[8388608]{0:T(1024)(128)(4,1)}), s8[4194304]{0:T(1024)(128)(4,1)S(1)}, s32[]{:S(2)}) async-start(s8[8388608]{0:T(1024)(128)(4,1)} %bitcast.41), calls=%async_computation.3 | async-start | bytes 8388608
  300.7 10.7 %collective-permute-start = (bf16[8,128,512]{2,1,0:T(8,128)(2,1)S(1)}, bf16[8,128,512]{2,1,0:T(8,128)(2,1)S(1)}, u32[]{:S(2)}, u32[]{:S(2)}) collective-permute-start(bf16[8,128,512]{2,1,0:T(8,128)(2,1)S(1)} %slice.13), channel_id=1, source_target_pairs={{0,1},{1,0},{2,3},{3,2},{4,5},{5,4},{6,7},{7,6}} | collective-permute-start | bytes 3145736 | tf_op jit(solution)/shard_map/ppermute | solution.py:548
  300.8 10.6 %copy-start.1 = (bf16[8,256,512]{2,1,0:T(8,128)(2,1)S(1)}, bf16[8,256,512]{2,1,0:T(8,128)(2,1)}, u32[]{:S(2)}) copy-start(bf16[8,256,512]{2,1,0:T(8,128)(2,1)} %get-tuple-element.16) | copy-start | bytes 6291460
where the time goes:
time: 703 us; the launch traced here: 694 us
  Pallas kernels  555 us (79%)
  local copies, waits for them, and re-layouts  80.1 us (11%)
  matrix products  53 us (8%)
    pallas_call x1, Pallas kernels, sum_all(): pl.pallas_call(functools.partial(sum_kernel, counts), out_shape=[jax.Shap...  327 us
    pallas_call x1, Pallas kernels, attention(): pl.pallas_call(functools.partial(attn_kernel, heads, hd, lag), grid=(ns,...  228 us
    unnamed x22, local copies, waits for them, and re-layouts  61.3 us
    dot_general x3, matrix products, local_step(): jnp.einsum(eq, x, w, preferred_element_type=F32).astype(BF16)  53 us
  transfers between devices with their start and end apart: 1, of which 0 were waited for; matrix products, arithmetic and copies ran while one was open for 2% of the time, Pallas kernels for 0%

commit v1 on v0

--- a/solution.py
+++ b/solution.py
@@ -45,9 +45,11 @@
     def _():
         for b in blocks:
             tab = slice(b * rows, (b + 1) * rows)
+            acc[b, s] = jnp.zeros_like(acc[b, s])
             k_rot[b] = rotate(kv[b, s, :, :hd], cos_ref[tab], sin_ref[tab], 1.0)
 
     keep = pos(lax.broadcasted_iota(jnp.int32, (rows, rows), 0)) >= pos(lax.broadcasted_iota(jnp.int32, (rows, rows), 1))
+    qs, dos, dss, pbs = [], [], [], []
     for h in range(heads):
         cols = slice(h * hd, (h + 1) * hd)
         wide = pl.ds(pl.multiple_of((step * heads + h) * hd, hd), hd)
@@ -69,22 +71,16 @@
         dq = rotate(dq, cos, sin, -1.0)
         stage[slot, 1, 0, :, wide] = dq[:half_rows]
         stage[slot, 1, 1, :, wide] = dq[half_rows:]
-        for i, b in enumerate(blocks):
-            dk = dot(ds[i], q, TN)
-            dv = dot(pb[i], do, TN)
-            if h == 0:
-                @pl.when(first)
-                def _():
-                    acc[b, s, :, :hd] = dk
-                    acc[b, s, :, hd:] = dv
-
-                @pl.when(jnp.logical_not(first))
-                def _():
-                    acc[b, s, :, :hd] += dk
-                    acc[b, s, :, hd:] += dv
-            else:
-                acc[b, s, :, :hd] += dk
-                acc[b, s, :, hd:] += dv
+        qs.append(q)
+        dos.append(do)
+        dss.append(ds)
+        pbs.append(pb)
+    q, do = jnp.concatenate(qs, axis=0), jnp.concatenate(dos, axis=0)
+    for i, b in enumerate(blocks):
+        dk = dot(jnp.concatenate([t[i] for t in dss], axis=0), q, TN)
+        dv = dot(jnp.concatenate([t[i] for t in pbs], axis=0), do, TN)
+        acc[b, s, :, :hd] += dk
+        acc[b, s, :, hd:] += dv
 
 
 MESH = pl.DeviceIdType.MESH
@@ -312,7 +308,7 @@
 
 
 def attn_kernel(heads, hd, lag, q_mine, do_mine, q_all, do_all, kv_all, cos_ref, sin_ref, o_out, dq_out, dkv_out,
-                kv, k_rot, q_in, do_in, stage, acc, relay, got, kv_mine_sem, pair_sem, kv_sem, in_sem, keep_sem, give_sem, one_sem, two_sem):
+                kv, k_rot, q_in, do_in, stage, acc, relay, got, kv_mine_sem, pair_sem, kv_sem, pass_sem, in_sem, keep_sem, give_sem, one_sem, two_sem):
     s, step = pl.program_id(0), pl.program_id(1)
     steps = pl.num_programs(1)
     ns, rows = kv.shape[1], kv.shape[2]
@@ -332,8 +328,11 @@
     def give_in(i, k):
         return remote((q_all, do_all)[k].at[yours + i], (q_in, do_in)[k].at[i], in_sem.at[k], i, partner)
 
-    up = (bit_x == 0, bit_y == 0, bit_y == 0)
-    down = (bit_x == 1, bit_y == 1, bit_y == 1)
+    up = ((bit_x == 0) | (chip == 1), bit_y == 0, chip == 0)
+    down = (bit_x == 1, bit_y == 1, chip == 3)
+
+    def pass_on(i):
+        return remote(kv.at[1, i], kv.at[3, i], pass_sem, i, dev_y)
 
     def pair():
         return remote(kv_all.at[pl.ds(yours, ns)], kv.at[0, :, pl.ds(half_rows, half_rows)], pair_sem, 0, partner)
@@ -356,8 +355,8 @@
 
         @pl.loop(0, ns)
         def _(i):
-            for b in (1, 2, 3):
-                @pl.when(up[b - 1])
+            for b, turn in ((1, up[0]), (2, chip == 1), (3, up[2])):
+                @pl.when(turn)
                 def _():
                     give_kv(b, i).start()
 
@@ -365,6 +364,14 @@
             def _():
                 for k in range(2):
                     give_in(i, k).start()
+
+        @pl.when(chip == 0)
+        def _():
+            @pl.loop(0, ns)
+            def _(i):
+                give_kv(2, i).start()
+                give_kv(1, i).wait_recv()
+                pass_on(i).start()
 
     def keep(i, k):
         return pltpu.make_async_copy(stage.at[i % 2, k, 0], (o_out, dq_out)[k].at[mine + i], keep_sem.at[k, i % 2])
@@ -380,6 +387,10 @@
             @pl.when(down[b - 1])
             def _():
                 give_kv(b, s).wait_recv()
+
+        @pl.when(chip == 2)
+        def _():
+            pass_on(s).wait_recv()
 
         @pl.when(s >= 2)
         def _():
@@ -472,6 +483,10 @@
                 @pl.when(up[b - 1])
                 def _():
                     give_kv(b, i).wait_send()
+
+            @pl.when(chip == 0)
+            def _():
+                pass_on(i).wait_send()
             for w in range(2):
                 @pl.when((bit_y == 1) & (i % 2 == w))
                 def _():
@@ -490,7 +505,7 @@
                 give(i, k).wait_send()
 
 
-def attention(q, do, kv, cos, sin, hd, heads=2, lag=1):
+def attention(q, do, kv, cos, sin, hd, heads=2, lag=2):
     batch, half_rows, width = q.shape
     ns, rows = batch // 2, 2 * half_rows
     mine = pl.BlockSpec((1, half_rows, heads * hd), lambda s, h: (lax.axis_index('sp') % 2 * ns + s, 0, h))
@@ -513,12 +528,40 @@
             pltpu.VMEM((4, ns, rows, 2 * hd), F32),
             pltpu.VMEM((ns, rows, 2 * hd), F32),
             pltpu.VMEM((2, ns, rows, 2 * hd), F32),
-            dma, dma((2, 1)), dma((3, 2, ns)), dma((2, 2, ns)), dma((2, 2)), dma((2, 2, ns)), dma((2, ns)), dma((2, 2, ns)),
+            dma, dma((2, 1)), dma((3, 2, ns)), dma((2, ns)), dma((2, 2, ns)), dma((2, 2)), dma((2, 2, ns)), dma((2, ns)), dma((2, 2, ns)),
         ],
         compiler_params=pltpu.CompilerParams(dimension_semantics=("arbitrary", "arbitrary"), collective_id=2, has_side_effects=True, vmem_limit_bytes=66 * 1000 * 1000),
         cost_estimate=pl.CostEstimate(flops=6 * 2 * ns * rows * width * rows * 4, bytes_accessed=100 * 1024 * 1024, transcendentals=0),
         name="attention",
     )(q, do, q, do, kv, cos, sin)
+
+
+def place_kernel(gwo, gwq, gwkv, a, d, wo, wq, wk, wv, a_out, d_out):
+    hd = wk.shape[1]
+    wo[...] = gwo[...]
+    for h in range(wq.shape[1]):
+        wq[:, h, :] = gwq[:, h * hd:(h + 1) * hd]
+    t = gwkv[...].T
+    wk[...] = t[:, :hd]
+    wv[...] = t[:, hd:]
+    a_out[...] = a[...]
+    d_out[...] = d[...]
+
+
+def place(gwo, gwq, gwkv, a, d, heads):
+    m, n = gwq.shape
+    hd = n // heads
+    tile = 128
+    rows = lambda w: pl.BlockSpec((tile, w), lambda i: (i, 0))
+    return pl.pallas_call(
+        place_kernel,
+        grid=(m // tile,),
+        in_specs=[rows(n), rows(n), pl.BlockSpec((2 * hd, tile), lambda i: (0, i)), rows(a.shape[1]), rows(d.shape[1])],
+        out_specs=[rows(n), pl.BlockSpec((tile, heads, hd), lambda i: (i, 0, 0)), rows(hd), rows(hd), rows(a.shape[1]), rows(d.shape[1])],
+        out_shape=[jax.ShapeDtypeStruct((m, n), F32), jax.ShapeDtypeStruct((m, heads, hd), F32), jax.ShapeDtypeStruct((m, hd), F32), jax.ShapeDtypeStruct((m, hd), F32), jax.ShapeDtypeStruct(a.shape, BF16), jax.ShapeDtypeStruct(d.shape, BF16)],
+        compiler_params=pltpu.CompilerParams(dimension_semantics=("arbitrary",), vmem_limit_bytes=40 * 1000 * 1000),
+        name="place",
+    )(gwo, gwq, gwkv, a, d)
 
 
 def solution(mesh):
@@ -532,7 +575,7 @@
         qw = w_query.shape[1] * hd
         dev = lax.axis_index('sp')
         core = dev % 2
-        wq = w_query.reshape(width, qw)
+        wq = lax.optimization_barrier(w_query.reshape(width, qw))
         wo = w_out.reshape(qw, width)
         wkv = jnp.concatenate([w_key, w_value], axis=1)
 
@@ -551,7 +594,7 @@
         dkv = jnp.concatenate([jnp.where(core == 0, dkv, dkv_back), jnp.where(core == 0, dkv_back, dkv)], axis=0)
         flat = lambda x: x.reshape(batch * local_len, -1)
         grad_wo, grad_wq, grad_wkv, attn_out, d_hidden = sum_all(flat(hidden), flat(d_out), flat(o), wo, flat(dq), wq, flat(dkv), wkv)
-        attn_out, d_hidden = attn_out.reshape(hidden.shape), d_hidden.reshape(hidden.shape)
-        return (attn_out, d_hidden, grad_wq.reshape(w_query.shape), grad_wkv[:hd].T, grad_wkv[hd:].T, grad_wo.reshape(w_out.shape))
+        grad_wo, grad_wq, grad_wk, grad_wv, attn_out, d_hidden = place(grad_wo, grad_wq, grad_wkv, attn_out, d_hidden, w_query.shape[1])
+        return (attn_out.reshape(hidden.shape), d_hidden.reshape(hidden.shape), grad_wq, grad_wk, grad_wv, grad_wo.reshape(w_out.shape))
 
     return jax.shard_map(local_step, mesh=mesh, in_specs=(seq_spec, seq_spec, rep_spec, rep_spec, rep_spec, rep_spec), out_specs=(seq_spec, seq_spec, rep_spec, rep_spec, rep_spec, rep_spec), check_vma=False)

time: 703 us -> 638 us (0.908); the launches traced: 694 us -> 637 us
  local copies, waits for them, and re-layouts: 80.1 us -> 18.9 us
    pallas_call x1, Pallas kernels: 228 us -> 182 us  [attention(): pl.pallas_call(functools.partial(attn_kernel, heads, hd, lag), grid=(ns,...]
    unnamed x22 -> x18, local copies, waits for them, and re-layouts: 61.3 us -> 17.4 us
    pallas_call x0 -> x1, Pallas kernels: none -> 34.9 us  [place(): pl.pallas_call(place_kernel, grid=(m // tile,), in_specs=[rows(n), rows(n...]
    reshape x1 -> x0, local copies, waits for them, and re-layouts: 13.5 us -> none  [local_step(): wq = w_query.reshape(width, qw)]
    pallas_call x1, Pallas kernels: 327 us -> 339 us  [sum_all(): pl.pallas_call(functools.partial(sum_kernel, counts), out_shape=[jax.Shap...]
  transfers between devices with their start and end apart: 1 -> 1, of which waited for: 0 -> 1; matrix products, arithmetic and copies ran while one was open for 2% -> 0% of each run, Pallas kernels for 0% -> 0%
where the time goes in v1:
time: 638 us; the launch traced here: 637 us
  Pallas kernels  556 us (87%)
  matrix products  53.3 us (8%)
  local copies, waits for them, and re-layouts  18.9 us (3%)
    pallas_call x1, Pallas kernels, sum_all(): pl.pallas_call(functools.partial(sum_kernel, counts), out_shape=[jax.Shap...  339 us
    pallas_call x1, Pallas kernels, attention(): pl.pallas_call(functools.partial(attn_kernel, heads, hd, lag), grid=(ns,...  182 us
    dot_general x3, matrix products, local_step(): jnp.einsum(eq, x, w, preferred_element_type=F32).astype(BF16)  53.3 us
    pallas_call x1, Pallas kernels, place(): pl.pallas_call(place_kernel, grid=(m // tile,), in_specs=[rows(n), rows(n...  34.9 us
    unnamed x18, local copies, waits for them, and re-layouts  17.4 us
  transfers between devices with their start and end apart: 1, of which 1 were waited for; matrix products, arithmetic and copies ran while one was open for 0% of the time, Pallas kernels for 0%

profile of v1, /device:TPU:0, one launch (start us, length us, event | category | flops | bytes accessed | tf_op | source)
XLA Modules:
  0.0 637.3 jit_solution(11371046585833496272)
XLA Ops:
  0.8 1.3 constant_dynamic-update-slice_fusion.1
  2.1 0.0 copy-start.3
  2.1 10.5 %copy.14 = bf16[256,8,8,256]{3,1,2,0:T(8,128)(2,1)} copy(bf16[256,8,8,256]{3,2,1,0:T(8,128)(2,1)} %bitcast.33) | data formatting | bytes 16777216
  12.7 0.0 copy-done.3
  12.7 0.0 slice-start
  12.7 0.0 slice-start.2
  12.7 0.1 constant_dynamic-update-slice_fusion.refs_7_
  12.8 0.0 copy-start.2
  12.8 0.0 slice-start.1
  12.8 0.0 slice-start.3
  12.8 10.2 %convert_bitcast_fusion.kv_all = bf16[16,128,512]{2,1,0:T(8,128)(2,1)} fusion(bf16[16,128,2048]{2,1,0:T(8,128)(2,1)} %param.6, bf16[2048,512]{1,0:T(8,128)(2,1)S(1)} %constant_dynamic-update-slice_fusion.refs_7_), kind=kOutput, calls=%fused_computation.7 | convolution fusion | flops 4296015872 | bytes 12582912 | tf_op jit(solution)/shard_map/bld,de->ble/dot_general | solution.py:586
  23.0 0.0 copy-done.2
  23.0 0.0 slice-done
  23.0 0.0 slice-done.2
  23.0 0.0 slice-done.1
  23.0 0.0 slice-done.3
  23.0 19.4 %fusion.2.q_mine.q_all = bf16[16,128,2048]{2,1,0:T(8,128)(2,1)} fusion(bf16[16,128,2048]{2,1,0:T(8,128)(2,1)S(1)} %bitcast.36, bf16[2048,2048]{1,0:T(8,128)(2,1)S(1)} %bitcast.32), kind=kOutput, calls=%fused_computation.2 | convolution fusion | flops 17184063488 | bytes 25165824 | tf_op jit(solution)/shard_map/bld,de->ble/dot_general | solution.py:586
  42.5 3.0 multiply_sine_fusion
  45.5 23.6 %convolution_convert_fusion.do_mine.do_all = bf16[16,128,2048]{2,1,0:T(8,128)(2,1)} fusion(bf16[16,128,2048]{2,1,0:T(8,128)(2,1)} %param.7, bf16[2048,2048,1]{1,0,2:T(8,128)(2,1)} %bitcast.38), kind=kOutput, calls=%fused_computation.3 | convolution fusion | flops 17184063488 | bytes 25165824 | tf_op jit(solution)/shard_map/bld,ed->ble/dot_general | solution.py:586
  69.1 182.0 %attention.1 = (bf16[16,128,2048]{2,1,0:T(8,128)(2,1)}, bf16[16,128,2048]{2,1,0:T(8,128)(2,1)}, bf16[8,256,512]{2,1,0:T(8,128)(2,1)}) custom-call(bf16[16,128,2048]{2,1,0:T(8,128)(2,1)} %fusion.2.q_mine.q_all, bf16[16,128,2048]{2,1,0:T(8,128)(2,1)} %convolution_convert_fusion.do_mine.do_all, bf16[16,128,2048]{2,1,0:T(8,128)(2,1)} %fusion.2.q_mine.q_all, ...), custom_call_target="tpu_custom_call" | custom-call | flops 51539607552 | bytes 104857600 | tf_op jit(solution)/shard_map/attention/pallas_call | solution.py:516
  251.1 1.3 slice.7
  252.5 0.0 collective-permute-start
  252.5 2.6 collective-permute-done
  255.2 1.4 broadcast_select_fusion.1
  256.5 1.5 pad_maximum_fusion
  258.0 338.8 %sum_all.1 = (f32[2048,2048]{1,0:T(8,128)}, f32[2048,2048]{1,0:T(8,128)}, f32[512,2048]{1,0:T(8,128)}, bf16[2048,2048]{1,0:T(8,128)(2,1)}, bf16[2048,2048]{1,0:T(8,128)(2,1)}, /*index=5*/f32[9,256,2048]{2,1,0:T(8,128)}) custom-call(bf16[2048,2048]{1,0:T(8,128)(2,1)} %bitcast.34, bf16[2048,2048]{1,0:T(8,128)(2,1)} %bitcast.37, bf16[2048,2048]{1,0:T(8,128)(2,1)} %bitcast.40, ...), custom_call_target="tpu_custom_call" | custom-call | tf_op jit(solution)/shard_map/sum_all/pallas_call | solution.py:286
  596.8 0.0 copy-start
  596.8 3.4 copy-done
  600.2 0.0 copy-start.1
  600.2 2.2 copy-done.1
  602.4 34.9 %place.1 = (f32[2048,2048]{1,0:T(8,128)}, f32[2048,8,256]{2,1,0:T(8,128)}, f32[2048,256]{1,0:T(8,128)}, f32[2048,256]{1,0:T(8,128)}, bf16[2048,2048]{1,0:T(8,128)(2,1)}, /*index=5*/bf16[2048,2048]{1,0:T(8,128)(2,1)}) custom-call(f32[2048,2048]{1,0:T(8,128)} %get-tuple-element.23.gwo, f32[2048,2048]{1,0:T(8,128)} %get-tuple-element.24.gwq, ...), custom_call_target="tpu_custom_call" | custom-call | tf_op jit(solution)/shard_map/place/pallas_call | solution.py:556
  (13 shorter events, 0.1 us)
Async XLA Ops:
  2.1 10.6 %copy-start.3 = (bf16[2048,256]{1,0:T(8,128)(2,1)S(1)}, bf16[2048,256]{1,0:T(8,128)(2,1)}, u32[]{:S(2)}) copy-start(bf16[2048,256]{1,0:T(8,128)(2,1)} %param.10) | copy-start | bytes 3145732
  12.7 10.3 %slice-start = ((s8[8388608]{0:T(1024)(128)(4,1)}), s8[4194304]{0:T(1024)(128)(4,1)S(1)}, s32[]{:S(2)}) async-start(s8[8388608]{0:T(1024)(128)(4,1)} %bitcast.30), calls=%async_computation | async-start | bytes 8388608
  12.7 10.3 %slice-start.2 = ((s8[8388608]{0:T(1024)(128)(4,1)}), s8[4194304]{0:T(1024)(128)(4,1)S(1)}, s32[]{:S(2)}) async-start(s8[8388608]{0:T(1024)(128)(4,1)} %bitcast.35), calls=%async_computation.2 | async-start | bytes 8388608
  12.8 10.2 %copy-start.2 = (bf16[2048,512]{1,0:T(8,128)(2,1)}, bf16[2048,512]{1,0:T(8,128)(2,1)S(1)}, u32[]{:S(2)}) copy-start(bf16[2048,512]{1,0:T(8,128)(2,1)S(1)} %constant_dynamic-update-slice_fusion.refs_7_) | copy-start | bytes 6291460
  12.8 10.2 %slice-start.1 = ((s8[8388608]{0:T(1024)(128)(4,1)}), s8[4194304]{0:T(1024)(128)(4,1)S(1)}, s32[]{:S(2)}) async-start(s8[8388608]{0:T(1024)(128)(4,1)} %bitcast.30), calls=%async_computation.1 | async-start | bytes 8388608
  12.8 10.2 %slice-start.3 = ((s8[8388608]{0:T(1024)(128)(4,1)}), s8[4194304]{0:T(1024)(128)(4,1)S(1)}, s32[]{:S(2)}) async-start(s8[8388608]{0:T(1024)(128)(4,1)} %bitcast.35), calls=%async_computation.3 | async-start | bytes 8388608
  252.5 2.7 collective-permute-start
  596.8 3.4 copy-start
  600.2 2.2 copy-start.1

commit v2 on v1

--- a/solution.py
+++ b/solution.py
@@ -95,7 +95,7 @@
     ng = len(counts)
     hid_ref, dout_ref, o_ref, wo_ref, dq_ref, wq_ref, dkv_ref, wkv_ref = refs[:8]
     out_refs, (attn_out, d_hidden, dr) = refs[8:ng + 8], refs[ng + 8:ng + 11]
-    h, dv, give, flip, r1, r2, xs, ws, xs2, ws2, tiles, dr_sem, mm_sem, tile_sem, keep_sem, d_sem, s1_sem, s2_sem, g1_sem, g2_sem, g3_sem = refs[ng + 11:]
+    h, dv, give, flip, r1, r2, xs, ws, xs2, ws2, tiles, early_sem, dr_sem, mm_sem, tile_sem, keep_sem, d_sem, s1_sem, s2_sem, g1_sem, g2_sem, g3_sem = refs[ng + 11:]
     total = sum(counts)
     dev = lax.axis_index('sp')
     chip, core = dev // 2, dev % 2
@@ -112,14 +112,14 @@
     def rows(ref, start, size):
         return ref.at[pl.ds(pl.multiple_of(start, 32), size)]
 
-    def each(body, which=range(ng)):
+    def each(body, which=range(ng), start=0):
         base = 0
         for i, count in enumerate(counts):
             def step(p, carry, i=i, base=base):
                 body(i, p, base + p)
                 return carry
             if i in which:
-                lax.fori_loop(0, count, step, 0)
+                lax.fori_loop(start, count, step, 0)
             base += count
 
     def cross(s):
@@ -256,8 +256,17 @@
         for copy in copies:
             copy.wait()
 
-    bring_all((o_ref, xs), (dout_ref, ws))
-    each(functools.partial(phase1, xs, ws), (0,))
+    blocks = [pl.ds(PIECE * k, PIECE) for k in range(counts[0])]
+    early = [pltpu.make_async_copy(src.at[:, at], dst.at[:, at], early_sem.at[g, k]) for k, at in enumerate(blocks) for g, (src, dst) in enumerate(((o_ref, xs), (dout_ref, ws)))]
+    for copy in early:
+        copy.start()
+    early[0].wait()
+    for copy in early[1::2]:
+        copy.wait()
+    phase1(xs, ws, 0, 0, 0)
+    for copy in early[2::2]:
+        copy.wait()
+    each(functools.partial(phase1, xs, ws), (0,), 1)
     bring_all((hid_ref, xs), (dq_ref, ws), (dkv_ref, xs2), (wkv_ref, ws2))
     each(functools.partial(phase1, xs, ws), (1,))
     each(functools.partial(phase1, xs2, xs), (2,))
@@ -298,7 +307,7 @@
             pltpu.VMEM(o.shape, BF16), pltpu.VMEM(wo.shape, BF16),
             pltpu.VMEM(dkv.shape, BF16), pltpu.VMEM(wkv.shape, BF16),
             pltpu.VMEM((2, 512, 256), BF16),
-            dma, dma((4,)), dma((2,)), dma((2, total)), dma((2, total)),
+            dma((2, counts[0])), dma, dma((4,)), dma((2,)), dma((2, total)), dma((2, total)),
             dma((2, 2, total)), dma((2, 2, total)), dma((2, 2, total)), dma((2, 2, total)), dma((2, total)),
         ],
         compiler_params=pltpu.CompilerParams(collective_id=1, has_side_effects=True, vmem_limit_bytes=67 * 1000 * 1000),
@@ -308,7 +317,7 @@
 
 
 def attn_kernel(heads, hd, lag, q_mine, do_mine, q_all, do_all, kv_all, cos_ref, sin_ref, o_out, dq_out, dkv_out,
-                kv, k_rot, q_in, do_in, stage, acc, relay, got, kv_mine_sem, pair_sem, kv_sem, pass_sem, in_sem, keep_sem, give_sem, one_sem, two_sem):
+                kv, k_rot, q_in, do_in, stage, acc, relay, got, dkv, kv_mine_sem, pair_sem, kv_sem, pass_sem, in_sem, keep_sem, give_sem, one_sem, two_sem, home_sem, back_sem):
     s, step = pl.program_id(0), pl.program_id(1)
     steps = pl.num_programs(1)
     ns, rows = kv.shape[1], kv.shape[2]
@@ -454,8 +463,16 @@
             two(i, 1).wait_recv()
             acc[0, i] += got[1, i]
         total = acc[0, i].astype(BF16)
-        dkv_out[i, :, :hd] = rotate(total[:, :hd], cos_ref[:rows], sin_ref[:rows], -1.0)
-        dkv_out[i, :, hd:] = total[:, hd:]
+        dkv[i, :, :hd] = rotate(total[:, :hd], cos_ref[:rows], sin_ref[:rows], -1.0)
+        dkv[i, :, hd:] = total[:, hd:]
+        home(i).start()
+        back(i).start()
+
+    def home(i):
+        return pltpu.make_async_copy(dkv.at[i, pl.ds(0, half_rows)], dkv_out.at[mine + i], home_sem.at[i])
+
+    def back(i):
+        return remote(dkv.at[i, pl.ds(half_rows, half_rows)], dkv_out.at[mine + i], back_sem, i, partner)
 
     @pl.when(step == steps - 1)
     def _():
@@ -499,6 +516,10 @@
             @pl.when(bit_y == 1)
             def _():
                 two(i, 1).wait_send()
+        @pl.loop(0, ns)
+        def _(i):
+            home(i).wait()
+            back(i).wait()
         for i in (ns - 2, ns - 1):
             for k in range(2):
                 keep(i, k).wait()
@@ -517,8 +538,8 @@
         functools.partial(attn_kernel, heads, hd, lag),
         grid=(ns, width // (heads * hd)),
         in_specs=[mine, mine, hbm, hbm, hbm, tab, tab],
-        out_specs=[hbm, hbm, pl.BlockSpec((ns, rows, 2 * hd), lambda s, h: (0, 0, 0))],
-        out_shape=[act, act, jax.ShapeDtypeStruct((ns, rows, 2 * hd), BF16)],
+        out_specs=[hbm, hbm, hbm],
+        out_shape=[act, act, jax.ShapeDtypeStruct(kv.shape, BF16)],
         scratch_shapes=[
             pltpu.VMEM((4, ns, rows, 2 * hd), BF16),
             pltpu.VMEM((4, rows, hd), BF16),
@@ -528,7 +549,8 @@
             pltpu.VMEM((4, ns, rows, 2 * hd), F32),
             pltpu.VMEM((ns, rows, 2 * hd), F32),
             pltpu.VMEM((2, ns, rows, 2 * hd), F32),
-            dma, dma((2, 1)), dma((3, 2, ns)), dma((2, ns)), dma((2, 2, ns)), dma((2, 2)), dma((2, 2, ns)), dma((2, ns)), dma((2, 2, ns)),
+            pltpu.VMEM((ns, rows, 2 * hd), BF16),
+            dma, dma((2, 1)), dma((3, 2, ns)), dma((2, ns)), dma((2, 2, ns)), dma((2, 2)), dma((2, 2, ns)), dma((2, ns)), dma((2, 2, ns)), dma((ns,)), dma((2, ns)),
         ],
         compiler_params=pltpu.CompilerParams(dimension_semantics=("arbitrary", "arbitrary"), collective_id=2, has_side_effects=True, vmem_limit_bytes=66 * 1000 * 1000),
         cost_estimate=pl.CostEstimate(flops=6 * 2 * ns * rows * width * rows * 4, bytes_accessed=100 * 1024 * 1024, transcendentals=0),
@@ -559,13 +581,12 @@
         in_specs=[rows(n), rows(n), pl.BlockSpec((2 * hd, tile), lambda i: (0, i)), rows(a.shape[1]), rows(d.shape[1])],
         out_specs=[rows(n), pl.BlockSpec((tile, heads, hd), lambda i: (i, 0, 0)), rows(hd), rows(hd), rows(a.shape[1]), rows(d.shape[1])],
         out_shape=[jax.ShapeDtypeStruct((m, n), F32), jax.ShapeDtypeStruct((m, heads, hd), F32), jax.ShapeDtypeStruct((m, hd), F32), jax.ShapeDtypeStruct((m, hd), F32), jax.ShapeDtypeStruct(a.shape, BF16), jax.ShapeDtypeStruct(d.shape, BF16)],
-        compiler_params=pltpu.CompilerParams(dimension_semantics=("arbitrary",), vmem_limit_bytes=40 * 1000 * 1000),
+        compiler_params=pltpu.CompilerParams(dimension_semantics=("arbitrary",), vmem_limit_bytes=66 * 1000 * 1000),
         name="place",
     )(gwo, gwq, gwkv, a, d)
 
 
 def solution(mesh):
-    n = mesh.shape['sp']
     seq_spec = P(None, 'sp', None)
     rep_spec = P()
 
@@ -574,10 +595,8 @@
         hd = w_key.shape[1]
         qw = w_query.shape[1] * hd
         dev = lax.axis_index('sp')
-        core = dev % 2
-        wq = lax.optimization_barrier(w_query.reshape(width, qw))
         wo = w_out.reshape(qw, width)
-        wkv = jnp.concatenate([w_key, w_value], axis=1)
+        wq, wkv = lax.optimization_barrier((w_query.reshape(width, qw), jnp.concatenate([w_key, w_value], axis=1)))
 
         offset = jnp.arange(local_len)
         positions = [((dev ^ (2 * b)) ^ c) * local_len + offset for b in range(4) for c in range(2)]
@@ -588,10 +607,7 @@
         do = proj(d_out, wo, 'bld,ed->ble')
         q = proj(hidden, wq, 'bld,de->ble')
         o, dq, dkv = attention(q, do, kv, cos, sin, hd)
-        dkv_back = lax.ppermute(dkv[:, local_len:], 'sp', [(d, d ^ 1) for d in range(n)])
-
-        dkv = dkv[:, :local_len]
-        dkv = jnp.concatenate([jnp.where(core == 0, dkv, dkv_back), jnp.where(core == 0, dkv_back, dkv)], axis=0)
+
         flat = lambda x: x.reshape(batch * local_len, -1)
         grad_wo, grad_wq, grad_wkv, attn_out, d_hidden = sum_all(flat(hidden), flat(d_out), flat(o), wo, flat(dq), wq, flat(dkv), wkv)
         grad_wo, grad_wq, grad_wk, grad_wv, attn_out, d_hidden = place(grad_wo, grad_wq, grad_wkv, attn_out, d_hidden, w_query.shape[1])

time: 638 us -> 631 us (0.989)
  local copies, waits for them, and re-layouts: 18.9 us -> 11.3 us
    unnamed x18 -> x9, local copies, waits for them, and re-layouts: 17.4 us -> 11.3 us
  transfers between devices with their start and end apart: 1 -> 0, of which waited for: 1 -> 0; matrix products, arithmetic and copies ran while one was open for 0% -> 0% of each run, Pallas kernels for 0% -> 0%
where the time goes in v2:
time: 631 us; the launch traced here: 630 us
  Pallas kernels  560 us (89%)
  matrix products  53.5 us (8%)
  local copies, waits for them, and re-layouts  11.3 us (2%)
    pallas_call x1, Pallas kernels, sum_all(): pl.pallas_call(functools.partial(sum_kernel, counts), out_shape=[jax.Shap...  339 us
    pallas_call x1, Pallas kernels, attention(): pl.pallas_call(functools.partial(attn_kernel, heads, hd, lag), grid=(ns,...  182 us
    dot_general x3, matrix products, local_step(): jnp.einsum(eq, x, w, preferred_element_type=F32).astype(BF16)  53.5 us
    pallas_call x1, Pallas kernels, place(): pl.pallas_call(place_kernel, grid=(m // tile,), in_specs=[rows(n), rows(n...  39 us

profile of v2, /device:TPU:0, one launch (start us, length us, event | category | flops | bytes accessed | tf_op | source)
XLA Modules:
  0.0 630.4 jit_solution(7565772081299404725)
XLA Ops:
  0.8 3.0 multiply_sine_fusion
  3.9 1.7 pad_maximum_fusion.refs_7_
  5.5 0.0 copy-start.1
  5.6 0.0 slice-start
  5.6 11.2 %copy.16 = bf16[256,8,8,256]{3,1,2,0:T(8,128)(2,1)} copy(bf16[256,8,8,256]{3,2,1,0:T(8,128)(2,1)} %bitcast.33) | data formatting | bytes 16777216
  16.8 0.0 copy-done.1
  16.8 0.0 copy-start
  16.8 0.0 slice-start.1
  16.8 9.2 %convert_bitcast_fusion.1.kv_all = bf16[16,128,512]{2,1,0:T(8,128)(2,1)} fusion(bf16[16,128,2048]{2,1,0:T(8,128)(2,1)} %param.6, bf16[2048,512]{1,0:T(8,128)(2,1)S(1)} %pad_maximum_fusion.refs_7_), kind=kOutput, calls=%fused_computation.7 | convolution fusion | flops 4296015872 | bytes 12582912 | tf_op jit(solution)/shard_map/bld,de->ble/dot_general | solution.py:605
  26.1 0.0 slice-done
  26.1 0.0 copy-done
  26.1 0.0 slice-done.1
  26.1 20.6 %convert_bitcast_fusion.q_mine.q_all = bf16[16,128,2048]{2,1,0:T(8,128)(2,1)} fusion(bf16[16,128,2048]{2,1,0:T(8,128)(2,1)S(1)} %bitcast.36, bf16[2048,2048]{1,0:T(8,128)(2,1)S(1)} %bitcast.32), kind=kOutput, calls=%fused_computation.2 | convolution fusion | flops 17184063488 | bytes 25165824 | tf_op jit(solution)/shard_map/bld,de->ble/dot_general | solution.py:605
  46.7 23.7 %convolution_convert_fusion.do_mine.do_all = bf16[16,128,2048]{2,1,0:T(8,128)(2,1)} fusion(bf16[16,128,2048]{2,1,0:T(8,128)(2,1)} %param.7, bf16[2048,2048,1]{1,0,2:T(8,128)(2,1)} %bitcast.38), kind=kOutput, calls=%fused_computation.3 | convolution fusion | flops 17184063488 | bytes 25165824 | tf_op jit(solution)/shard_map/bld,ed->ble/dot_general | solution.py:605
  70.4 181.8 %attention.1 = (bf16[16,128,2048]{2,1,0:T(8,128)(2,1)}, bf16[16,128,2048]{2,1,0:T(8,128)(2,1)}, bf16[16,128,512]{2,1,0:T(8,128)(2,1)}) custom-call(bf16[16,128,2048]{2,1,0:T(8,128)(2,1)} %convert_bitcast_fusion.q_mine.q_all, bf16[16,128,2048]{2,1,0:T(8,128)(2,1)} %convolution_convert_fusion.do_mine.do_all, ...), custom_call_target="tpu_custom_call" | custom-call | flops 51539607552 | bytes 104857600 | tf_op jit(solution)/shard_map/attention/pallas_call | solution.py:537
  252.2 339.2 %sum_all.1 = (f32[2048,2048]{1,0:T(8,128)}, f32[2048,2048]{1,0:T(8,128)}, f32[512,2048]{1,0:T(8,128)}, bf16[2048,2048]{1,0:T(8,128)(2,1)}, bf16[2048,2048]{1,0:T(8,128)(2,1)}, /*index=5*/f32[9,256,2048]{2,1,0:T(8,128)}) custom-call(bf16[2048,2048]{1,0:T(8,128)(2,1)} %bitcast.34, bf16[2048,2048]{1,0:T(8,128)(2,1)} %bitcast.37, bf16[2048,2048]{1,0:T(8,128)(2,1)} %bitcast.40, ...), custom_call_target="tpu_custom_call" | custom-call | tf_op jit(solution)/shard_map/sum_all/pallas_call | solution.py:295
  591.5 39.0 %place.1 = (f32[2048,2048]{1,0:T(8,128)}, f32[2048,8,256]{2,1,0:T(8,128)}, f32[2048,256]{1,0:T(8,128)}, f32[2048,256]{1,0:T(8,128)}, bf16[2048,2048]{1,0:T(8,128)(2,1)}, /*index=5*/bf16[2048,2048]{1,0:T(8,128)(2,1)}) custom-call(f32[2048,2048]{1,0:T(8,128)} %get-tuple-element.27.gwo, f32[2048,2048]{1,0:T(8,128)} %get-tuple-element.28.gwq, ...), custom_call_target="tpu_custom_call" | custom-call | tf_op jit(solution)/shard_map/place/pallas_call | solution.py:578
  (12 shorter events, 0.1 us)
Async XLA Ops:
  5.5 11.3 %copy-start.1 = (bf16[2048,512]{1,0:T(8,128)(2,1)}, bf16[2048,512]{1,0:T(8,128)(2,1)S(1)}, u32[]{:S(2)}) copy-start(bf16[2048,512]{1,0:T(8,128)(2,1)S(1)} %pad_maximum_fusion.refs_7_) | copy-start | bytes 6291460
  5.6 20.5 %slice-start = ((s8[8388608]{0:T(1024)(128)(4,1)}), s8[4194304]{0:T(1024)(128)(4,1)S(1)}, s32[]{:S(2)}) async-start(s8[8388608]{0:T(1024)(128)(4,1)} %bitcast.35), calls=%async_computation | async-start | bytes 8388608
  16.8 9.3 %copy-start = (bf16[256,8,8,256]{3,1,2,0:T(8,128)(2,1)S(1)}, bf16[256,8,8,256]{3,1,2,0:T(8,128)(2,1)}, u32[]{:S(2)}) copy-start(bf16[256,8,8,256]{3,1,2,0:T(8,128)(2,1)} %copy.16) | copy-start | bytes 25165828
  16.8 9.3 %slice-start.1 = ((s8[8388608]{0:T(1024)(128)(4,1)}), s8[4194304]{0:T(1024)(128)(4,1)S(1)}, s32[]{:S(2)}) async-start(s8[8388608]{0:T(1024)(128)(4,1)} %bitcast.35), calls=%async_computation.1 | async-start | bytes 8388608
